TPU v7x, 32 devices: a whole 2x2x4 slice. The times are simulated.
32 devices in a mesh: sy: 8 (over y, x, core), sx: 4 (over z).
Axes of the slice: x: 2, y: 2, z: 4, core: 2. Of those that a mesh axis runs over, the one named last changes fastest.
Arguments:
- spectrum: bfloat16 [2, 9216, 9216], P(None, 'sy', 'sx'), may hold values from -6 to 6
- pupils: bfloat16 [2, 2048, 2048], P(None, 'sy', 'sx'), may hold values from -6 to 6
- amplitudes: float32 [8, 8, 4, 256, 256], P('sy', 'sx'), may hold values from 0.2 to 2
- crop_starts: int32 [8, 8, 4, 2], P('sy', 'sx'), may hold values from 0 to 896
- led_counts: int32 [8, 8], P('sy', 'sx'), may hold values from 1 to 4, as said below
Outputs:
- spectrum_grad: bfloat16 [2, 9216, 9216], P(None, 'sy', 'sx')
- pupil_grad: float32 [2, 2048, 2048], P(None, 'sy', 'sx')
Inputs may be any that keep to these rules, and one draw needn't show every extreme that they name: `led_counts`: slots at or past a segment's count are ignored.
All inputs are finite; a program needn't handle non-finite values.
Results may differ from a plain program's by a relative error of at most 0.001.
Values may be sent and summed in bfloat16 or wider, within the bound.
A program may use at most 256 MiB of HBM per device.

v0:
```python
import functools
import math

import jax
import jax.numpy as jnp
import numpy as np
from jax import lax
from jax.experimental import pallas as pl
from jax.experimental.pallas import tpu as pltpu
from jax.sharding import PartitionSpec as P

H = 64
MAXL = 4
LANES = 128
CH = 32
SUB = 16
FLOOR_SQUARE = 0.0625
MU_WEIGHT = 0.5
LAM_WEIGHT = 0.5
F32 = jnp.float32
BF16 = jnp.bfloat16

def half_tables(side):
    half = side // 2
    n = np.arange(half)[:, None]
    k = np.arange(half)[None, :]
    mats = []
    for odd in (0, 1):
        ang = 2.0 * math.pi * ((n * (2 * k + odd)) % side) / side
        re, im = np.cos(ang) / math.sqrt(side), np.sin(ang) / math.sqrt(side)
        right = np.block([[re, im], [-im, re]])
        mats += [right, right.T]
    mats = np.stack(mats).astype(np.float32)
    hi = mats.astype(jnp.bfloat16)
    lo = (mats - hi.astype(np.float32)).astype(jnp.bfloat16)
    perm = np.zeros((side, side), np.float32)
    perm[2 * np.arange(half), np.arange(half)] = 1.0
    perm[2 * np.arange(half) + 1, half + np.arange(half)] = 1.0
    return np.concatenate([hi, lo, perm.astype(jnp.bfloat16)[None]])


def split(value):
    hi = value.astype(BF16)
    return hi, (value - hi.astype(F32)).astype(BF16)


def dot(a, b):
    return jnp.dot(a, b, preferred_element_type=F32)


def window_of(start_ref, seg, slot, edge, win_r, win_c):
    base = (seg * MAXL + slot) * 2
    a = start_ref[base]
    b = start_ref[base + 1]
    a_al = jnp.minimum(a // SUB * SUB, edge - win_r)
    b_al = jnp.minimum(b // LANES * LANES, edge - win_c)
    return a, b, a_al, b_al


def crop_kernel(start_ref, count_ref, spec, crops, win, wf, in_sem):
    pw = crops.shape[2]
    edge = spec.shape[1]
    cols_dev = spec.shape[2] // edge
    win_r, win_c = win.shape[2], win.shape[3]
    win_t = win_c // LANES

    def fetch(seg, slot, buf):
        _, _, a_al, b_al = window_of(start_ref, seg, slot, edge, win_r, win_c)
        rs = pl.multiple_of(a_al, SUB)
        cs = pl.multiple_of(seg * edge + b_al, LANES)
        return pltpu.make_async_copy(
            spec.at[:, pl.ds(rs, win_r), pl.ds(cs, win_c)], win.at[buf], in_sem.at[buf]
        )

    fetch(0, 0, 0).start()

    def slot_step(seg, slot, count):
        buf = lax.rem(count, 2)
        more = slot + 1 < count_ref[seg]
        nseg = jnp.where(more, seg, seg + 1)
        nslot = jnp.where(more, slot + 1, 0)

        @pl.when(nseg < cols_dev)
        def _():
            fetch(nseg, nslot, 1 - buf).start()

        fetch(seg, slot, buf).wait()
        a, b, a_al, b_al = window_of(start_ref, seg, slot, edge, win_r, win_c)
        a_off = a - a_al
        for p in range(2):
            for r in range(0, win_r, SUB):
                wide = win[buf, p, r : r + SUB, :].astype(F32)
                for t in range(win_t):
                    wf[p, t, r : r + SUB, :] = wide[:, t * LANES : (t + 1) * LANES]
        back_roll = lax.rem(win_c - (b - b_al), win_c)
        for r in range(0, pw, CH):
            for p in range(2):
                wide = jnp.concatenate(
                    [wf[p, t, pl.ds(a_off + r, CH), :] for t in range(win_t)], axis=1
                )
                crops[seg * MAXL + slot, p, r : r + CH, :] = pltpu.roll(
                    wide, back_roll, axis=1
                )[:, :pw].astype(BF16)
        return count + 1

    def segment(seg, count):
        return lax.fori_loop(
            0, count_ref[seg], lambda slot, c: slot_step(seg, slot, c), count
        )

    lax.fori_loop(0, cols_dev, segment, jnp.int32(0))


def wave_kernel(
    spec, pup_hbm, amps, crops, pup, tab,
    backs, up, down, west, east, pup_up, pup_down, pup_west, pup_east, nw, ne, sw, se,
    ampbuf, xs, ys, ampp, in_sem, send_sem, recv_sem,
):
    pw = pup.shape[1]
    half = pw // 2
    edge = spec.shape[1]
    width = spec.shape[2]
    pwide = pup.shape[2]
    band = 2 * H
    total = crops.shape[0]
    iy, ix = lax.axis_index("sy"), lax.axis_index("sx")
    ny, nx = lax.axis_size("sy"), lax.axis_size("sx")
    has = {}
    for dy in (-1, 0, 1):
        for dx in (-1, 0, 1):
            ok = (iy + dy >= 0) & (iy + dy < ny) & (ix + dx >= 0) & (ix + dx < nx)
            has[dy, dx] = ok

    barrier = pltpu.get_barrier_semaphore()
    near = [(dy, dx) for dy in (-1, 0, 1) for dx in (-1, 0, 1) if dy or dx]
    for dy, dx in near:
        @pl.when(has[dy, dx])
        def _(dy=dy, dx=dx):
            pl.semaphore_signal(
                barrier, inc=1, device_id=(iy + dy, ix + dx),
                device_id_type=pl.DeviceIdType.MESH,
            )
    pl.semaphore_wait(barrier, sum(has[d].astype(jnp.int32) for d in near))
    tops, bots = slice(0, band), slice(edge - band, edge)
    lefts, rights = slice(0, band), slice(width - band, width)
    moves = [
        ((1, 0), spec.at[:, bots, :], up),
        ((-1, 0), spec.at[:, tops, :], down),
        ((0, 1), spec.at[:, :, rights], west),
        ((0, -1), spec.at[:, :, lefts], east),
        ((1, 0), pup_hbm, pup_up),
        ((-1, 0), pup_hbm, pup_down),
        ((0, 1), pup_hbm.at[:, :, pwide - pw :], pup_west),
        ((0, -1), pup_hbm.at[:, :, :pw], pup_east),
        ((1, 1), spec.at[:, bots, rights], nw),
        ((1, -1), spec.at[:, bots, lefts], ne),
        ((-1, 1), spec.at[:, tops, rights], sw),
        ((-1, -1), spec.at[:, tops, lefts], se),
    ]
    copies = []
    for n, ((dy, dx), src, dst) in enumerate(moves):
        copies.append(
            pltpu.make_async_remote_copy(
                src_ref=src, dst_ref=dst, send_sem=send_sem.at[n], recv_sem=recv_sem.at[n],
                device_id=(iy + dy, ix + dx), device_id_type=pl.DeviceIdType.MESH,
            )
        )
    for c, ((dy, dx), _, _) in zip(copies, moves):
        @pl.when(has[dy, dx])
        def _(c=c):
            c.start()

    def put(which, rows, cols, value):
        hi, lo = split(value)
        xs[which, 0, rows, cols] = hi
        xs[which, 1, rows, cols] = lo

    def from_right(which, table):
        lhs = jnp.concatenate([xs[which, 0], xs[which, 1], xs[which, 0]], axis=1)
        rhs = jnp.concatenate([tab[table], tab[table], tab[4 + table]], axis=0)
        ys[which] = dot(lhs, rhs)

    def from_left(which, table):
        rhs = jnp.concatenate([xs[which, 0], xs[which, 1], xs[which, 0]], axis=0)
        lhs = jnp.concatenate([tab[table], tab[table], tab[4 + table]], axis=1)
        ys[which] = dot(lhs, rhs)

    lo_c, hi_c, all_c = slice(0, half), slice(half, pw), slice(0, pw)

    def fetch(i, buf):
        seg = lax.div(i, MAXL)
        slot = lax.rem(i, MAXL)
        return [
            pltpu.make_async_copy(
                amps.at[seg, slot, :, t * LANES : (t + 1) * LANES],
                ampbuf.at[buf, t],
                in_sem.at[t, buf],
            )
            for t in range(pw // LANES)
        ]

    for c in fetch(0, 0):
        c.start()

    def slot_step(i, _):
        buf = lax.rem(i, 2)

        @pl.when(i + 1 < total)
        def _():
            for c in fetch(i + 1, 1 - buf):
                c.start()

        for c in fetch(i, buf):
            c.wait()
        pc = pl.multiple_of(lax.div(i, MAXL) * pw, LANES)
        for r in range(0, pw, CH):
            rows = slice(r, r + CH)
            cre = crops[i, 0, rows, :].astype(F32)
            cim = crops[i, 1, rows, :].astype(F32)
            pre = pup[0, rows, pl.ds(pc, pw)].astype(F32)
            pim = pup[1, rows, pl.ds(pc, pw)].astype(F32)
            fre = pre * cre - pim * cim
            fim = pre * cim + pim * cre
            put(0, rows, lo_c, fre[:, lo_c] + fre[:, hi_c])
            put(0, rows, hi_c, fim[:, lo_c] + fim[:, hi_c])
            put(1, rows, lo_c, fre[:, lo_c] - fre[:, hi_c])
            put(1, rows, hi_c, fim[:, lo_c] - fim[:, hi_c])
        from_right(0, 0)
        from_right(1, 2)
        for r in range(0, half, CH):
            for part, cols in ((0, lo_c), (1, hi_c)):
                rows = slice(part * half + r, part * half + r + CH)
                for which, ocols in ((0, lo_c), (1, hi_c)):
                    upper = ys[which, r : r + CH, cols]
                    lower = ys[which, half + r : half + r + CH, cols]
                    put(2, rows, ocols, upper + lower)
                    put(3, rows, ocols, upper - lower)
        ahi, alo = [], []
        for odd in range(2):
            h, l = split(
                jnp.concatenate(
                    [ampbuf[buf, t, pl.ds(odd, half, stride=2), :] for t in range(pw // LANES)],
                    axis=1,
                )
            )
            ahi.append(h)
            alo.append(l)
        lhs = jnp.concatenate(
            [jnp.concatenate(ahi, axis=0), jnp.concatenate(alo, axis=0)], axis=1
        )
        ampp[...] = dot(lhs, jnp.concatenate([tab[8], tab[8]], axis=0))
        from_left(2, 1)
        from_left(3, 3)
        for which in range(2):
            for r in range(0, half, CH):
                re = ys[2 + which, r : r + CH, :]
                im = ys[2 + which, half + r : half + r + CH, :]
                amp = ampp[which * half + r : which * half + r + CH, :]
                keep = 1.0 - amp * lax.rsqrt(jnp.maximum(re * re + im * im, FLOOR_SQUARE))
                put(which, slice(r, r + CH), all_c, re * keep)
                put(which, slice(half + r, half + r + CH), all_c, im * keep)
        from_left(0, 0)
        from_left(1, 2)
        for r in range(0, half, CH):
            for part, cols in ((0, lo_c), (1, hi_c)):
                even = ys[0, part * half + r : part * half + r + CH, :]
                odd = ys[1, part * half + r : part * half + r + CH, :]
                upper, lower = even + odd, even - odd
                for rows, val in (
                    (slice(r, r + CH), upper), (slice(half + r, half + r + CH), lower),
                ):
                    put(2, rows, cols, val[:, lo_c])
                    put(3, rows, cols, val[:, hi_c])
        from_right(2, 1)
        from_right(3, 3)
        for r in range(0, pw, CH):
            rows = slice(r, r + CH)
            even, odd = ys[2, rows, :], ys[3, rows, :]
            plus, minus = even + odd, even - odd
            backs[i, 0, rows, lo_c] = plus[:, lo_c]
            backs[i, 0, rows, hi_c] = minus[:, lo_c]
            backs[i, 1, rows, lo_c] = plus[:, hi_c]
            backs[i, 1, rows, hi_c] = minus[:, hi_c]
        return 0

    lax.fori_loop(0, total, slot_step, 0)
    for c, ((dy, dx), _, _) in zip(copies, moves):
        @pl.when(has[dy, dx])
        def _(c=c):
            c.wait_send()

        @pl.when(has[-dy, -dx])
        def _(c=c):
            c.wait_recv()


def finish_kernel(
    start_ref, count_ref, flag_ref, spec, pup, crops, backs,
    up, down, west, east, pup_up, pup_down, pup_west, pup_east, nw, ne, sw, se,
    out, pgrad,
    acc, stage, rows_buf, sides, hrows, hsides, hcorn, hpv, hph, band_sem, out_sem,
):
    pw = pup.shape[1]
    edge = spec.shape[1]
    cols_dev = spec.shape[2] // edge
    band = 2 * H
    win_r, win_c = pw + SUB, pw + LANES
    win_t = win_c // LANES
    last = edge // LANES - 1
    w_top, w_bot, w_left, w_right = (flag_ref[i] for i in range(4))
    loads = [
        (spec.at[:, 0:band, :], rows_buf.at[0]),
        (spec.at[:, edge - band :, :], rows_buf.at[1]),
    ]
    for s in range(cols_dev):
        for j, c0 in enumerate((s * edge, (s + 1) * edge - band)):
            loads.append((spec.at[:, :, c0 : c0 + band], sides.at[2 * s + j]))
    loads += [
        (up, hrows.at[0]), (down, hrows.at[1]), (west, hsides.at[0]), (east, hsides.at[1]),
        (nw, hcorn.at[0]), (ne, hcorn.at[1]), (sw, hcorn.at[2]), (se, hcorn.at[3]),
        (pup_up, hpv.at[0]), (pup_down, hpv.at[1]), (pup_west, hph.at[0]), (pup_east, hph.at[1]),
    ]
    loads = [
        pltpu.make_async_copy(src, dst, band_sem.at[n]) for n, (src, dst) in enumerate(loads)
    ]
    for c in loads:
        c.start()

    def zero_acc(seg):
        def zero(i, _):
            r = pl.multiple_of(i * 8, 8)
            for p in range(2):
                for t in range(edge // LANES):
                    acc[seg, p, t, pl.ds(r, 8), :] = jnp.zeros((8, LANES), F32)
            return 0

        lax.fori_loop(0, edge // 8, zero, 0)
        for p in range(2):
            pgrad[p, :, pl.ds(pl.multiple_of(seg * pw, LANES), pw)] = jnp.zeros((pw, pw), F32)

    def own_terms(seg):
        wl = jnp.where(seg == 0, w_left, 1.0)
        wr = jnp.where(seg == cols_dev - 1, w_right, 1.0)
        il = jnp.where(seg == 0, 0.0, 1.0)
        ir = jnp.where(seg == cols_dev - 1, 0.0, 1.0)
        lo_nb = jnp.maximum(2 * seg - 1, 0)
        hi_nb = jnp.minimum(2 * seg + 2, 2 * cols_dev - 1)
        cbase = pl.multiple_of(seg * edge, LANES)

        def side(i, _):
            r = pl.multiple_of(i * SUB, SUB)
            vert = 1.0 + jnp.where(r < band, w_top, 0.0) + jnp.where(r >= edge - band, w_bot, 0.0)
            for p in range(2):
                mine = sides[2 * seg, p, pl.ds(r, SUB), :].astype(F32)
                other = sides[lo_nb, p, pl.ds(r, SUB), :].astype(F32)
                acc[seg, p, 0, pl.ds(r, SUB), :] += MU_WEIGHT * (wl * vert * mine - il * other)
                mine = sides[2 * seg + 1, p, pl.ds(r, SUB), :].astype(F32)
                other = sides[hi_nb, p, pl.ds(r, SUB), :].astype(F32)
                acc[seg, p, last, pl.ds(r, SUB), :] += MU_WEIGHT * (
                    wr * vert * mine - ir * other
                )
            return 0

        lax.fori_loop(0, edge // SUB, side, 0)

        def flat(i, _):
            r = pl.multiple_of(i * SUB, SUB)
            for p in range(2):
                for j, w in ((0, w_top), (1, w_bot)):
                    mine = rows_buf[j, p, pl.ds(r, SUB), pl.ds(cbase, edge)].astype(F32)
                    rs = pl.ds(pl.multiple_of(r + j * (edge - band), SUB), SUB)
                    for t in range(edge // LANES):
                        acc[seg, p, t, rs, :] += (MU_WEIGHT * w) * mine[
                            :, t * LANES : (t + 1) * LANES
                        ]
            return 0

        lax.fori_loop(0, band // SUB, flat, 0)
        pc = pl.multiple_of(seg * pw, LANES)
        pl_c = pl.multiple_of(jnp.maximum(seg - 1, 0) * pw, LANES)
        pr_c = pl.multiple_of(jnp.minimum(seg + 1, cols_dev - 1) * pw, LANES)
        near = w_top + w_bot + wl + wr

        def pups(i, _):
            r = pl.multiple_of(i * SUB, SUB)
            for p in range(2):
                mine = pup[p, pl.ds(r, SUB), pl.ds(pc, pw)].astype(F32)
                lef = pup[p, pl.ds(r, SUB), pl.ds(pl_c, pw)].astype(F32)
                rig = pup[p, pl.ds(r, SUB), pl.ds(pr_c, pw)].astype(F32)
                pgrad[p, pl.ds(r, SUB), pl.ds(pc, pw)] += LAM_WEIGHT * (
                    near * mine - il * lef - ir * rig
                )
            return 0

        lax.fori_loop(0, pw // SUB, pups, 0)

    def halo_terms(seg):
        def rows_part(j, edge_row):
            def step(i, _):
                r = pl.multiple_of(i * SUB, SUB)
                rs = pl.ds(pl.multiple_of(r + edge_row, SUB), SUB)
                for p in range(2):
                    cb = pl.multiple_of(seg * edge, LANES)
                    wide = hrows[j, p, pl.ds(r, SUB), pl.ds(cb, edge)].astype(F32)
                    for t in range(last + 1):
                        acc[seg, p, t, rs, :] -= MU_WEIGHT * wide[:, t * LANES : (t + 1) * LANES]
                return 0

            lax.fori_loop(0, band // SUB, step, 0)

            def corner(t, fetch):
                for p in range(2):
                    for r in range(0, band, SUB):
                        rs = slice(edge_row + r, edge_row + r + SUB)
                        acc[seg, p, t, rs, :] -= MU_WEIGHT * fetch(p, slice(r, r + SUB)).astype(F32)

            @pl.when(seg > 0)
            def _():
                c0 = pl.multiple_of(seg * edge - LANES, LANES)
                corner(0, lambda p, r: hrows[j, p, r, pl.ds(c0, LANES)])

            @pl.when(seg < cols_dev - 1)
            def _():
                c0 = pl.multiple_of((seg + 1) * edge, LANES)
                corner(last, lambda p, r: hrows[j, p, r, pl.ds(c0, LANES)])

            @pl.when((seg == 0) & (w_left > 0.0))
            def _():
                corner(0, lambda p, r: hcorn[2 * j, p, r, :])

            @pl.when((seg == cols_dev - 1) & (w_right > 0.0))
            def _():
                corner(last, lambda p, r: hcorn[2 * j + 1, p, r, :])

            pc = pl.multiple_of(seg * pw, LANES)
            for p in range(2):
                for r in range(0, pw, CH):
                    rows = slice(r, r + CH)
                    pgrad[p, rows, pl.ds(pc, pw)] -= LAM_WEIGHT * hpv[
                        j, p, rows, pl.ds(pc, pw)
                    ].astype(F32)

        def cols_part(j, t):
            def step(i, _):
                rs = pl.ds(pl.multiple_of(i * CH, CH), CH)
                for p in range(2):
                    acc[seg, p, t, rs, :] -= MU_WEIGHT * hsides[j, p, rs, :].astype(F32)
                return 0

            lax.fori_loop(0, edge // CH, step, 0)
            pc = pl.multiple_of(seg * pw, LANES)
            for p in range(2):
                for r in range(0, pw, CH):
                    rows = slice(r, r + CH)
                    pgrad[p, rows, pl.ds(pc, pw)] -= LAM_WEIGHT * hph[j, p, rows, :].astype(F32)

        @pl.when(w_top > 0.0)
        def _():
            rows_part(0, 0)

        @pl.when(w_bot > 0.0)
        def _():
            rows_part(1, edge - band)

        @pl.when((seg == 0) & (w_left > 0.0))
        def _():
            cols_part(0, 0)

        @pl.when((seg == cols_dev - 1) & (w_right > 0.0))
        def _():
            cols_part(1, last)

    def slot_step(seg, slot):
        a, b, _, b_al = window_of(start_ref, seg, slot, edge, win_r, win_c)
        b_off = b - b_al
        tile0 = b_al // LANES
        pc = pl.multiple_of(seg * pw, LANES)
        n = seg * MAXL + slot
        for r in range(0, pw, CH):
            rows = slice(r, r + CH)
            bre, bim = backs[n, 0, rows, :], backs[n, 1, rows, :]
            pre = pup[0, rows, pl.ds(pc, pw)].astype(F32)
            pim = pup[1, rows, pl.ds(pc, pw)].astype(F32)
            cre, cim = crops[n, 0, rows, :].astype(F32), crops[n, 1, rows, :].astype(F32)
            pgrad[0, rows, pl.ds(pc, pw)] += cre * bre + cim * bim
            pgrad[1, rows, pl.ds(pc, pw)] += cre * bim - cim * bre
            blank = jnp.zeros((CH, win_c - pw), F32)
            for p, val in ((0, pre * bre + pim * bim), (1, pre * bim - pim * bre)):
                wide = pltpu.roll(jnp.concatenate([val, blank], axis=1), b_off, axis=1)
                for t in range(win_t):
                    acc[seg, p, tile0 + t, pl.ds(a + r, CH), :] += wide[
                        :, t * LANES : (t + 1) * LANES
                    ]

    def put_out(seg):
        cb = pl.multiple_of(seg * edge, LANES)
        return pltpu.make_async_copy(
            stage.at[seg], out.at[:, :, pl.ds(cb, edge)], out_sem.at[seg]
        )

    def segment(seg, _):
        zero_acc(seg)

        @pl.when(seg == 0)
        def _():
            for c in loads:
                c.wait()

        own_terms(seg)
        halo_terms(seg)

        def one(slot, _):
            slot_step(seg, slot)
            return 0

        lax.fori_loop(0, count_ref[seg], one, 0)

        def conv(i, _):
            rs = pl.ds(pl.multiple_of(i * SUB, SUB), SUB)
            for p in range(2):
                for t in range(edge // LANES):
                    stage[seg, p, rs, t * LANES : (t + 1) * LANES] = acc[
                        seg, p, t, rs, :
                    ].astype(BF16)
            return 0

        lax.fori_loop(0, edge // SUB, conv, 0)
        put_out(seg).start()
        return 0

    lax.fori_loop(0, cols_dev, segment, 0)
    for s in range(cols_dev):
        put_out(s).wait()


def local(spectrum, pupils, amplitudes, crop_starts, led_counts):
    cols_dev = amplitudes.shape[1]
    total = cols_dev * MAXL
    pw = pupils.shape[1]
    edge = spectrum.shape[1]
    width = spectrum.shape[2]
    pwide = pupils.shape[2]
    band = 2 * H
    iy, ix = lax.axis_index("sy"), lax.axis_index("sx")
    flags = jnp.stack(
        [iy > 0, iy < lax.axis_size("sy") - 1, ix > 0, ix < lax.axis_size("sx") - 1]
    ).astype(F32)
    table = jnp.asarray(half_tables(pw))
    smem = pl.BlockSpec(memory_space=pltpu.SMEM)
    vmem = pl.BlockSpec(memory_space=pltpu.VMEM)
    hbm = pl.BlockSpec(memory_space=pltpu.HBM)
    win_r, win_c = pw + SUB, pw + LANES
    starts = crop_starts.reshape(-1)
    counts = led_counts.reshape(-1)
    sds = jax.ShapeDtypeStruct
    crops = pl.pallas_call(
        crop_kernel,
        out_shape=sds((total, 2, pw, pw), BF16),
        in_specs=[smem, smem, hbm],
        out_specs=vmem,
        scratch_shapes=[
            pltpu.VMEM((2, 2, win_r, win_c), BF16),
            pltpu.VMEM((2, win_c // LANES, win_r, LANES), F32),
            pltpu.SemaphoreType.DMA((2,)),
        ],
        compiler_params=pltpu.CompilerParams(vmem_limit_bytes=16 * 2**20),
        name="crops",
    )(starts, counts, spectrum)
    rows_s, cols_s = sds((2, band, width), BF16), sds((2, edge, band), BF16)
    pv_s, ph_s, corner_s = sds(pupils.shape, BF16), sds((2, pw, pw), BF16), sds((2, band, band), BF16)
    halos = (rows_s, rows_s, cols_s, cols_s, pv_s, pv_s, ph_s, ph_s) + (corner_s,) * 4
    backs, *around = pl.pallas_call(
        wave_kernel,
        out_shape=(sds((total, 2, pw, pw), F32),) + halos,
        in_specs=[hbm, hbm, hbm, vmem, vmem, vmem],
        out_specs=(vmem,) + (hbm,) * len(halos),
        scratch_shapes=[
            pltpu.VMEM((2, pw // LANES, pw, LANES), F32),
            pltpu.VMEM((4, 2, pw, pw), BF16),
            pltpu.VMEM((4, pw, pw), F32),
            pltpu.VMEM((pw, pw), F32),
            pltpu.SemaphoreType.DMA((pw // LANES, 2)),
            pltpu.SemaphoreType.DMA((len(halos),)),
            pltpu.SemaphoreType.DMA((len(halos),)),
        ],
        compiler_params=pltpu.CompilerParams(
            vmem_limit_bytes=24 * 2**20, collective_id=0, has_side_effects=True
        ),
        name="waves",
    )(spectrum, pupils, amplitudes[0], crops, pupils, table)
    return pl.pallas_call(
        finish_kernel,
        out_shape=(sds(spectrum.shape, BF16), sds(pupils.shape, F32)),
        in_specs=[smem, smem, smem, hbm, vmem, vmem, vmem] + [hbm] * len(halos),
        out_specs=(hbm, vmem),
        scratch_shapes=[
            pltpu.VMEM((cols_dev, 2, edge // LANES, edge, LANES), F32),
            pltpu.VMEM((cols_dev, 2, edge, edge), BF16),
            pltpu.VMEM((2, 2, band, width), BF16),
            pltpu.VMEM((2 * cols_dev, 2, edge, band), BF16),
            pltpu.VMEM((2,) + rows_s.shape, BF16),
            pltpu.VMEM((2,) + cols_s.shape, BF16),
            pltpu.VMEM((4,) + corner_s.shape, BF16),
            pltpu.VMEM((2,) + pv_s.shape, BF16),
            pltpu.VMEM((2,) + ph_s.shape, BF16),
            pltpu.SemaphoreType.DMA((2 + 2 * cols_dev + len(halos),)),
            pltpu.SemaphoreType.DMA((cols_dev,)),
        ],
        compiler_params=pltpu.CompilerParams(vmem_limit_bytes=52 * 2**20),
        name="finish",
    )(starts, counts, flags, spectrum, pupils, crops, backs, *around)


def solution(mesh):
    placed = (
        P(None, "sy", "sx"),
        P(None, "sy", "sx"),
        P("sy", "sx", None, None, None),
        P("sy", "sx", None, None),
        P("sy", "sx"),
    )
    return jax.shard_map(
        local,
        mesh=mesh,
        in_specs=placed,
        out_specs=(P(None, "sy", "sx"), P(None, "sy", "sx")),
        check_vma=False,
    )
```

profile of v0, /device:TPU:12, one launch (start us, length us, event | category | flops | bytes accessed | tf_op | source)
XLA Modules:
  0.0 92.1 jit_solution(196249991452306788)
XLA Ops:
  0.6 0.1 add_convert_fusion.flag_ref
  0.7 0.8 copy.9
  1.5 0.1 reshape.10.start_ref
  1.6 4.0 %copy-done = bf16[2,1152,2304]{2,1,0:T(8,128)(2,1)S(1)} copy-done((bf16[2,1152,2304]{2,1,0:T(8,128)(2,1)S(1)}, bf16[2,1152,2304]{2,1,0:T(8,128)(2,1)}, u32[]{:S(2)}) %copy-start) | copy-done | bytes 10616856
  5.6 0.7 copy-done.23
  6.3 2.1 %crops.1 = bf16[8,2,256,256]{3,2,1,0:T(8,128)(2,1)S(1)} custom-call(s32[16]{0:T(128)S(1)} %reshape.10.start_ref, s32[2]{0:T(128)S(1)} %bitcast.7, bf16[2,1152,2304]{2,1,0:T(8,128)(2,1)S(1)} %copy-done), custom_call_target="tpu_custom_call" | custom-call | tf_op jit(solution)/shard_map/crops/pallas_call | solution.py:556
  8.4 1.9 %copy-done.1 = bf16[2,1152,2304]{2,1,0:T(8,128)(2,1)S(1)} copy-done((bf16[2,1152,2304]{2,1,0:T(8,128)(2,1)S(1)}, bf16[2,1152,2304]{2,1,0:T(8,128)(2,1)}, u32[]{:S(2)}) %copy-start.1) | copy-done | bytes 10616856
  10.3 0.1 copy-done.3
  10.4 0.3 copy-done.7
  10.7 1.6 %copy-done.6 = f32[1,2,4,256,256]{4,3,2,1,0:T(8,128)S(1)} copy-done((f32[1,2,4,256,256]{4,3,2,1,0:T(8,128)S(1)}, f32[1,2,4,256,256]{4,3,2,1,0:T(8,128)}, u32[]{:S(2)}) %copy-start.6) | copy-done | bytes 2097176
  12.3 44.1 %waves.1 = (f32[8,2,256,256]{3,2,1,0:T(8,128)S(1)}, bf16[2,128,2304]{2,1,0:T(8,128)(2,1)S(1)}, bf16[2,128,2304]{2,1,0:T(8,128)(2,1)S(1)}, bf16[2,1152,128]{2,1,0...) custom-call(bf16[2,1152,2304]{2,1,0:T(8,128)(2,1)S(1)} %copy-done.1,, ...), custom_call_target="tpu_custom_call" | custom-call | tf_op jit(solution)/shard_map/waves/pallas_call | solution.py:572
  56.4 0.0 copy-done.2
  56.5 0.0 copy-start.5
  56.5 1.9 %copy-done.5 = f32[8,2,256,256]{3,2,1,0:T(8,128)} copy-done((f32[8,2,256,256]{3,2,1,0:T(8,128)}, f32[8,2,256,256]{3,2,1,0:T(8,128)S(1)}, u32[]{:S(2)}) %copy-start.5) | copy-done | bytes 4194328
  58.4 1.0 %copy-done.8 = bf16[2,128,2304]{2,1,0:T(8,128)(2,1)} copy-done((bf16[2,128,2304]{2,1,0:T(8,128)(2,1)}, bf16[2,128,2304]{2,1,0:T(8,128)(2,1)S(1)}, u32[]{:S(2)}) %copy-start.8) | copy-done | bytes 1179672
  59.4 1.1 %copy-done.9 = bf16[2,128,2304]{2,1,0:T(8,128)(2,1)} copy-done((bf16[2,128,2304]{2,1,0:T(8,128)(2,1)}, bf16[2,128,2304]{2,1,0:T(8,128)(2,1)S(1)}, u32[]{:S(2)}) %copy-start.9) | copy-done | bytes 1179672
  60.5 0.9 copy-done.10
  61.4 0.8 copy-done.11
  62.2 0.8 copy-done.12
  63.0 0.8 copy-done.14
  63.9 0.7 copy-done.15
  64.6 0.7 copy-done.17
  65.3 0.6 copy-done.19
  65.9 0.6 copy-done.21
  66.5 0.0 copy-done.4
  66.5 0.0 copy-done.24
  66.5 1.0 %copy-done.13 = bf16[2,256,512]{2,1,0:T(8,128)(2,1)S(1)} copy-done((bf16[2,256,512]{2,1,0:T(8,128)(2,1)S(1)}, bf16[2,256,512]{2,1,0:T(8,128)(2,1)}, u32[]{:S(2)}) %copy-start.13) | copy-done | bytes 524312
  67.6 0.9 %copy-done.16 = bf16[2,256,256]{2,1,0:T(8,128)(2,1)S(1)} copy-done((bf16[2,256,256]{2,1,0:T(8,128)(2,1)S(1)}, bf16[2,256,256]{2,1,0:T(8,128)(2,1)}, u32[]{:S(2)}) %copy-start.16) | copy-done | bytes 262168
  68.5 0.9 %copy-done.18 = bf16[2,256,256]{2,1,0:T(8,128)(2,1)S(1)} copy-done((bf16[2,256,256]{2,1,0:T(8,128)(2,1)S(1)}, bf16[2,256,256]{2,1,0:T(8,128)(2,1)}, u32[]{:S(2)}) %copy-start.18) | copy-done | bytes 262168
  69.5 0.8 copy-done.20
  70.3 0.8 copy-done.22
  71.2 20.9 %finish.1 = (bf16[2,1152,2304]{2,1,0:T(8,128)(2,1)}, f32[2,256,512]{2,1,0:T(8,128)}) custom-call(s32[16]{0:T(128)S(1)} %reshape.10.start_ref, s32[2]{0:T(128)S(1)} %bitcast.8, f32[4]{0:T(128)S(1)} %add_convert_fusion.flag_ref, bf16[2,1152,2304]{2,1,0:T(8,128)(2,1)} %spec.5, bf16[2,256,512]{2,1,0:T(8,128)(2,1)S(1)} %copy-done.4, ...), custom_call_target="tpu_custom_call" | custom-call | tf_op jit(solution)/shard_map/finish/pallas_call | solution.py:591
  (24 shorter events, 0.0 us)
Async XLA Ops:
  1.6 4.0 %copy-start = (bf16[2,1152,2304]{2,1,0:T(8,128)(2,1)S(1)}, bf16[2,1152,2304]{2,1,0:T(8,128)(2,1)}, u32[]{:S(2)}) copy-start(bf16[2,1152,2304]{2,1,0:T(8,128)(2,1)} %spec.5) | copy-start | bytes 31850500
  5.6 0.7 copy-start.23
  6.3 4.0 %copy-start.1 = (bf16[2,1152,2304]{2,1,0:T(8,128)(2,1)S(1)}, bf16[2,1152,2304]{2,1,0:T(8,128)(2,1)}, u32[]{:S(2)}) copy-start(bf16[2,1152,2304]{2,1,0:T(8,128)(2,1)} %spec.5) | copy-start | bytes 31850500
  6.3 4.2 %copy-start.3 = (bf16[2,256,512]{2,1,0:T(8,128)(2,1)S(1)}, bf16[2,256,512]{2,1,0:T(8,128)(2,1)}, u32[]{:S(2)}) copy-start(bf16[2,256,512]{2,1,0:T(8,128)(2,1)} %pup.3) | copy-start | bytes 1572868
  6.3 4.4 %copy-start.7 = (bf16[9,256,256]{2,1,0:T(8,128)(2,1)S(1)}, bf16[9,256,256]{2,1,0:T(8,128)(2,1)}, u32[]{:S(2)}) copy-start(bf16[9,256,256]{2,1,0:T(8,128)(2,1)} %constant.17.clone.tab) | copy-start | bytes 3538948
  10.7 1.6 %copy-start.6 = (f32[1,2,4,256,256]{4,3,2,1,0:T(8,128)S(1)}, f32[1,2,4,256,256]{4,3,2,1,0:T(8,128)}, u32[]{:S(2)}) copy-start(f32[1,2,4,256,256]{4,3,2,1,0:T(8,128)} %param.8) | copy-start | bytes 6291460
  12.3 44.2 %copy-start.2 = (bf16[8,2,256,256]{3,2,1,0:T(8,128)(2,1)}, bf16[8,2,256,256]{3,2,1,0:T(8,128)(2,1)S(1)}, u32[]{:S(2)}) copy-start(bf16[8,2,256,256]{3,2,1,0:T(8,128)(2,1)S(1)} %crops.1) | copy-start | bytes 6291460
  12.3 54.2 %copy-start.4 = (bf16[2,256,512]{2,1,0:T(8,128)(2,1)S(1)}, bf16[2,256,512]{2,1,0:T(8,128)(2,1)}, u32[]{:S(2)}) copy-start(bf16[2,256,512]{2,1,0:T(8,128)(2,1)} %pup.3) | copy-start | bytes 1572868
  12.3 54.2 %copy-start.24 = (s32[1,2]{1,0:T(1,128)S(1)}, s32[1,2]{1,0:T(1,128)}, u32[]{:S(2)}) copy-start(s32[1,2]{1,0:T(1,128)} %param.10) | copy-start | bytes 28
  56.5 1.9 %copy-start.5 = (f32[8,2,256,256]{3,2,1,0:T(8,128)}, f32[8,2,256,256]{3,2,1,0:T(8,128)S(1)}, u32[]{:S(2)}) copy-start(f32[8,2,256,256]{3,2,1,0:T(8,128)S(1)} %get-tuple-element.15.backs) | copy-start | bytes 12582916
  58.4 1.0 %copy-start.8 = (bf16[2,128,2304]{2,1,0:T(8,128)(2,1)}, bf16[2,128,2304]{2,1,0:T(8,128)(2,1)S(1)}, u32[]{:S(2)}) copy-start(bf16[2,128,2304]{2,1,0:T(8,128)(2,1)S(1)} %get-tuple-element.16.up) | copy-start | bytes 3538948
  59.4 1.1 %copy-start.9 = (bf16[2,128,2304]{2,1,0:T(8,128)(2,1)}, bf16[2,128,2304]{2,1,0:T(8,128)(2,1)S(1)}, u32[]{:S(2)}) copy-start(bf16[2,128,2304]{2,1,0:T(8,128)(2,1)S(1)} %get-tuple-element.17.down) | copy-start | bytes 3538948
  60.5 0.9 copy-start.10
  61.4 0.8 copy-start.11
  62.2 0.8 copy-start.12
  63.0 0.8 copy-start.14
  63.9 0.7 copy-start.15
  64.6 0.7 copy-start.17
  65.3 0.6 copy-start.19
  65.9 0.6 copy-start.21
  66.5 1.0 %copy-start.13 = (bf16[2,256,512]{2,1,0:T(8,128)(2,1)S(1)}, bf16[2,256,512]{2,1,0:T(8,128)(2,1)}, u32[]{:S(2)}) copy-start(bf16[2,256,512]{2,1,0:T(8,128)(2,1)} %copy-done.12) | copy-start | bytes 1572868
  67.6 0.9 %copy-start.16 = (bf16[2,256,256]{2,1,0:T(8,128)(2,1)S(1)}, bf16[2,256,256]{2,1,0:T(8,128)(2,1)}, u32[]{:S(2)}) copy-start(bf16[2,256,256]{2,1,0:T(8,128)(2,1)} %copy-done.15) | copy-start | bytes 786436
  68.5 0.9 %copy-start.18 = (bf16[2,256,256]{2,1,0:T(8,128)(2,1)S(1)}, bf16[2,256,256]{2,1,0:T(8,128)(2,1)}, u32[]{:S(2)}) copy-start(bf16[2,256,256]{2,1,0:T(8,128)(2,1)} %copy-done.17) | copy-start | bytes 786436
  69.5 0.8 copy-start.20
  70.3 0.8 copy-start.22
where the time goes:
time: 92.5 us; the launch traced here: 92.1 us
  Pallas kernels  67.1 us (73%)
  local copies, waits for them, and re-layouts  24.1 us (26%)
    pallas_call x1, Pallas kernels, local(): pl.pallas_call(wave_kernel, out_shape=(sds((total, 2, pw, pw), F32),) + h...  44.1 us
    unnamed x51, local copies, waits for them, and re-layouts  24.1 us
    pallas_call x1, Pallas kernels, local(): pl.pallas_call(finish_kernel, out_shape=(sds(spectrum.shape, BF16), sds(p...  20.9 us
    pallas_call x1, Pallas kernels, local(): pl.pallas_call(crop_kernel, out_shape=sds((total, 2, pw, pw), BF16), in_s...  2.09 us

commit v1 on v0

--- a/solution.py
+++ b/solution.py
@@ -13,6 +13,7 @@
 MAXL = 4
 LANES = 128
 CH = 32
+GRANT = 62 * 2**20
 SUB = 16
 FLOOR_SQUARE = 0.0625
 MU_WEIGHT = 0.5
@@ -112,9 +113,9 @@
 
 
 def wave_kernel(
-    spec, pup_hbm, amps, crops, pup, tab,
-    backs, up, down, west, east, pup_up, pup_down, pup_west, pup_east, nw, ne, sw, se,
-    ampbuf, xs, ys, ampp, in_sem, send_sem, recv_sem,
+    count_ref, flag_ref, spec, pup_hbm, amps, crops, pup, tab,
+    pgrad, backs, up, down, west, east, pup_up, pup_down, pup_west, pup_east, nw, ne, sw, se,
+    ampbuf, cbuf, obuf, xs, ys, ampp, in_sem, back_sem, send_sem, recv_sem,
 ):
     pw = pup.shape[1]
     half = pw // 2
@@ -197,10 +198,41 @@
                 in_sem.at[t, buf],
             )
             for t in range(pw // LANES)
-        ]
+        ] + [pltpu.make_async_copy(crops.at[i], cbuf.at[buf], in_sem.at[pw // LANES, buf])]
+
+    def give(i, buf):
+        return pltpu.make_async_copy(obuf.at[buf], backs.at[i], back_sem.at[buf])
 
     for c in fetch(0, 0):
         c.start()
+    cols_dev = width // edge
+    w_top, w_bot, w_left, w_right = (flag_ref[k] for k in range(4))
+
+    def own_pup(seg, _):
+        wl = jnp.where(seg == 0, w_left, 1.0)
+        wr = jnp.where(seg == cols_dev - 1, w_right, 1.0)
+        il = jnp.where(seg == 0, 0.0, 1.0)
+        ir = jnp.where(seg == cols_dev - 1, 0.0, 1.0)
+        pc = pl.multiple_of(seg * pw, LANES)
+        pl_c = pl.multiple_of(jnp.maximum(seg - 1, 0) * pw, LANES)
+        pr_c = pl.multiple_of(jnp.minimum(seg + 1, cols_dev - 1) * pw, LANES)
+        near = w_top + w_bot + wl + wr
+
+        def pups(i, _):
+            r = pl.multiple_of(i * SUB, SUB)
+            for p in range(2):
+                mine = pup[p, pl.ds(r, SUB), pl.ds(pc, pw)].astype(F32)
+                lef = pup[p, pl.ds(r, SUB), pl.ds(pl_c, pw)].astype(F32)
+                rig = pup[p, pl.ds(r, SUB), pl.ds(pr_c, pw)].astype(F32)
+                pgrad[p, pl.ds(r, SUB), pl.ds(pc, pw)] = LAM_WEIGHT * (
+                    near * mine - il * lef - ir * rig
+                )
+            return 0
+
+        lax.fori_loop(0, pw // SUB, pups, 0)
+        return 0
+
+    lax.fori_loop(0, cols_dev, own_pup, 0)
 
     def slot_step(i, _):
         buf = lax.rem(i, 2)
@@ -215,8 +247,8 @@
         pc = pl.multiple_of(lax.div(i, MAXL) * pw, LANES)
         for r in range(0, pw, CH):
             rows = slice(r, r + CH)
-            cre = crops[i, 0, rows, :].astype(F32)
-            cim = crops[i, 1, rows, :].astype(F32)
+            cre = cbuf[buf, 0, rows, :].astype(F32)
+            cim = cbuf[buf, 1, rows, :].astype(F32)
             pre = pup[0, rows, pl.ds(pc, pw)].astype(F32)
             pim = pup[1, rows, pl.ds(pc, pw)].astype(F32)
             fre = pre * cre - pim * cim
@@ -273,17 +305,31 @@
                     put(3, rows, cols, val[:, hi_c])
         from_right(2, 1)
         from_right(3, 3)
+        @pl.when(i >= 2)
+        def _():
+            give(i - 2, buf).wait()
+
+        live = jnp.full((CH, pw), lax.rem(i, MAXL), jnp.int32) < count_ref[lax.div(i, MAXL)]
         for r in range(0, pw, CH):
             rows = slice(r, r + CH)
             even, odd = ys[2, rows, :], ys[3, rows, :]
             plus, minus = even + odd, even - odd
-            backs[i, 0, rows, lo_c] = plus[:, lo_c]
-            backs[i, 0, rows, hi_c] = minus[:, lo_c]
-            backs[i, 1, rows, lo_c] = plus[:, hi_c]
-            backs[i, 1, rows, hi_c] = minus[:, hi_c]
+            bre = jnp.concatenate([plus[:, lo_c], minus[:, lo_c]], axis=1)
+            bim = jnp.concatenate([plus[:, hi_c], minus[:, hi_c]], axis=1)
+            pre = pup[0, rows, pl.ds(pc, pw)].astype(F32)
+            pim = pup[1, rows, pl.ds(pc, pw)].astype(F32)
+            cre = cbuf[buf, 0, rows, :].astype(F32)
+            cim = cbuf[buf, 1, rows, :].astype(F32)
+            obuf[buf, 0, rows, :] = pre * bre + pim * bim
+            obuf[buf, 1, rows, :] = pre * bim - pim * bre
+            pgrad[0, rows, pl.ds(pc, pw)] += jnp.where(live, cre * bre + cim * bim, 0.0)
+            pgrad[1, rows, pl.ds(pc, pw)] += jnp.where(live, cre * bim - cim * bre, 0.0)
+        give(i, buf).start()
         return 0
 
     lax.fori_loop(0, total, slot_step, 0)
+    for i in range(max(total - 2, 0), total):
+        give(i, i % 2).wait()
     for c, ((dy, dx), _, _) in zip(copies, moves):
         @pl.when(has[dy, dx])
         def _(c=c):
@@ -295,12 +341,12 @@
 
 
 def finish_kernel(
-    start_ref, count_ref, flag_ref, spec, pup, crops, backs,
+    start_ref, count_ref, flag_ref, spec, pgrad_in, backs_hbm,
     up, down, west, east, pup_up, pup_down, pup_west, pup_east, nw, ne, sw, se,
     out, pgrad,
-    acc, stage, rows_buf, sides, hrows, hsides, hcorn, hpv, hph, band_sem, out_sem,
+    acc, stage, backs, rows_buf, sides, hrows, hsides, hcorn, hpv, hph, band_sem, out_sem,
 ):
-    pw = pup.shape[1]
+    pw = pgrad.shape[1]
     edge = spec.shape[1]
     cols_dev = spec.shape[2] // edge
     band = 2 * H
@@ -319,6 +365,7 @@
         (up, hrows.at[0]), (down, hrows.at[1]), (west, hsides.at[0]), (east, hsides.at[1]),
         (nw, hcorn.at[0]), (ne, hcorn.at[1]), (sw, hcorn.at[2]), (se, hcorn.at[3]),
         (pup_up, hpv.at[0]), (pup_down, hpv.at[1]), (pup_west, hph.at[0]), (pup_east, hph.at[1]),
+        (backs_hbm, backs),
     ]
     loads = [
         pltpu.make_async_copy(src, dst, band_sem.at[n]) for n, (src, dst) in enumerate(loads)
@@ -335,8 +382,6 @@
             return 0
 
         lax.fori_loop(0, edge // 8, zero, 0)
-        for p in range(2):
-            pgrad[p, :, pl.ds(pl.multiple_of(seg * pw, LANES), pw)] = jnp.zeros((pw, pw), F32)
 
     def own_terms(seg):
         wl = jnp.where(seg == 0, w_left, 1.0)
@@ -376,23 +421,6 @@
             return 0
 
         lax.fori_loop(0, band // SUB, flat, 0)
-        pc = pl.multiple_of(seg * pw, LANES)
-        pl_c = pl.multiple_of(jnp.maximum(seg - 1, 0) * pw, LANES)
-        pr_c = pl.multiple_of(jnp.minimum(seg + 1, cols_dev - 1) * pw, LANES)
-        near = w_top + w_bot + wl + wr
-
-        def pups(i, _):
-            r = pl.multiple_of(i * SUB, SUB)
-            for p in range(2):
-                mine = pup[p, pl.ds(r, SUB), pl.ds(pc, pw)].astype(F32)
-                lef = pup[p, pl.ds(r, SUB), pl.ds(pl_c, pw)].astype(F32)
-                rig = pup[p, pl.ds(r, SUB), pl.ds(pr_c, pw)].astype(F32)
-                pgrad[p, pl.ds(r, SUB), pl.ds(pc, pw)] += LAM_WEIGHT * (
-                    near * mine - il * lef - ir * rig
-                )
-            return 0
-
-        lax.fori_loop(0, pw // SUB, pups, 0)
 
     def halo_terms(seg):
         def rows_part(j, edge_row):
@@ -474,18 +502,12 @@
         a, b, _, b_al = window_of(start_ref, seg, slot, edge, win_r, win_c)
         b_off = b - b_al
         tile0 = b_al // LANES
-        pc = pl.multiple_of(seg * pw, LANES)
         n = seg * MAXL + slot
         for r in range(0, pw, CH):
             rows = slice(r, r + CH)
-            bre, bim = backs[n, 0, rows, :], backs[n, 1, rows, :]
-            pre = pup[0, rows, pl.ds(pc, pw)].astype(F32)
-            pim = pup[1, rows, pl.ds(pc, pw)].astype(F32)
-            cre, cim = crops[n, 0, rows, :].astype(F32), crops[n, 1, rows, :].astype(F32)
-            pgrad[0, rows, pl.ds(pc, pw)] += cre * bre + cim * bim
-            pgrad[1, rows, pl.ds(pc, pw)] += cre * bim - cim * bre
             blank = jnp.zeros((CH, win_c - pw), F32)
-            for p, val in ((0, pre * bre + pim * bim), (1, pre * bim - pim * bre)):
+            for p in range(2):
+                val = backs[n, p, rows, :]
                 wide = pltpu.roll(jnp.concatenate([val, blank], axis=1), b_off, axis=1)
                 for t in range(win_t):
                     acc[seg, p, tile0 + t, pl.ds(a + r, CH), :] += wide[
@@ -498,14 +520,13 @@
             stage.at[seg], out.at[:, :, pl.ds(cb, edge)], out_sem.at[seg]
         )
 
+    for s in range(cols_dev):
+        zero_acc(s)
+    pgrad[...] = pgrad_in[...]
+    for c in loads:
+        c.wait()
+
     def segment(seg, _):
-        zero_acc(seg)
-
-        @pl.when(seg == 0)
-        def _():
-            for c in loads:
-                c.wait()
-
         own_terms(seg)
         halo_terms(seg)
 
@@ -563,39 +584,43 @@
             pltpu.VMEM((2, win_c // LANES, win_r, LANES), F32),
             pltpu.SemaphoreType.DMA((2,)),
         ],
-        compiler_params=pltpu.CompilerParams(vmem_limit_bytes=16 * 2**20),
+        compiler_params=pltpu.CompilerParams(vmem_limit_bytes=GRANT),
         name="crops",
     )(starts, counts, spectrum)
     rows_s, cols_s = sds((2, band, width), BF16), sds((2, edge, band), BF16)
     pv_s, ph_s, corner_s = sds(pupils.shape, BF16), sds((2, pw, pw), BF16), sds((2, band, band), BF16)
     halos = (rows_s, rows_s, cols_s, cols_s, pv_s, pv_s, ph_s, ph_s) + (corner_s,) * 4
-    backs, *around = pl.pallas_call(
+    pgrad, backs, *around = pl.pallas_call(
         wave_kernel,
-        out_shape=(sds((total, 2, pw, pw), F32),) + halos,
-        in_specs=[hbm, hbm, hbm, vmem, vmem, vmem],
-        out_specs=(vmem,) + (hbm,) * len(halos),
+        out_shape=(sds(pupils.shape, F32), sds((total, 2, pw, pw), F32)) + halos,
+        in_specs=[smem, smem, hbm, hbm, hbm, hbm, vmem, vmem],
+        out_specs=(vmem, hbm) + (hbm,) * len(halos),
         scratch_shapes=[
             pltpu.VMEM((2, pw // LANES, pw, LANES), F32),
+            pltpu.VMEM((2, 2, pw, pw), BF16),
+            pltpu.VMEM((2, 2, pw, pw), F32),
             pltpu.VMEM((4, 2, pw, pw), BF16),
             pltpu.VMEM((4, pw, pw), F32),
             pltpu.VMEM((pw, pw), F32),
-            pltpu.SemaphoreType.DMA((pw // LANES, 2)),
+            pltpu.SemaphoreType.DMA((1 + pw // LANES, 2)),
+            pltpu.SemaphoreType.DMA((2,)),
             pltpu.SemaphoreType.DMA((len(halos),)),
             pltpu.SemaphoreType.DMA((len(halos),)),
         ],
         compiler_params=pltpu.CompilerParams(
-            vmem_limit_bytes=24 * 2**20, collective_id=0, has_side_effects=True
+            vmem_limit_bytes=GRANT, collective_id=0, has_side_effects=True
         ),
         name="waves",
-    )(spectrum, pupils, amplitudes[0], crops, pupils, table)
+    )(counts, flags, spectrum, pupils, amplitudes[0], crops, pupils, table)
     return pl.pallas_call(
         finish_kernel,
         out_shape=(sds(spectrum.shape, BF16), sds(pupils.shape, F32)),
-        in_specs=[smem, smem, smem, hbm, vmem, vmem, vmem] + [hbm] * len(halos),
+        in_specs=[smem, smem, smem, hbm, vmem, hbm] + [hbm] * len(halos),
         out_specs=(hbm, vmem),
         scratch_shapes=[
             pltpu.VMEM((cols_dev, 2, edge // LANES, edge, LANES), F32),
             pltpu.VMEM((cols_dev, 2, edge, edge), BF16),
+            pltpu.VMEM((total, 2, pw, pw), F32),
             pltpu.VMEM((2, 2, band, width), BF16),
             pltpu.VMEM((2 * cols_dev, 2, edge, band), BF16),
             pltpu.VMEM((2,) + rows_s.shape, BF16),
@@ -603,12 +628,12 @@
             pltpu.VMEM((4,) + corner_s.shape, BF16),
             pltpu.VMEM((2,) + pv_s.shape, BF16),
             pltpu.VMEM((2,) + ph_s.shape, BF16),
-            pltpu.SemaphoreType.DMA((2 + 2 * cols_dev + len(halos),)),
+            pltpu.SemaphoreType.DMA((3 + 2 * cols_dev + len(halos),)),
             pltpu.SemaphoreType.DMA((cols_dev,)),
         ],
-        compiler_params=pltpu.CompilerParams(vmem_limit_bytes=52 * 2**20),
+        compiler_params=pltpu.CompilerParams(vmem_limit_bytes=GRANT),
         name="finish",
-    )(starts, counts, flags, spectrum, pupils, crops, backs, *around)
+    )(starts, counts, flags, spectrum, pgrad, backs, *around)
 
 
 def solution(mesh):

time: 92.5 us -> 73.6 us (0.80)
  local copies, waits for them, and re-layouts: 24.1 us -> 1.34 us
  Pallas kernels: 67.1 us -> 70.7 us
    unnamed x51 -> x1, local copies, waits for them, and re-layouts: 24.1 us -> 0.77 us
    pallas_call x1, Pallas kernels: 2.09 us -> 6.12 us  [local(): pl.pallas_call(crop_kernel, out_shape=sds((total, 2, pw, pw), BF16), in_s...]
    pallas_call x1, Pallas kernels: 20.9 us -> 18.9 us  [local(): pl.pallas_call(finish_kernel, out_shape=(sds(spectrum.shape, BF16), sds(p...]
    pallas_call x1, Pallas kernels: 44.1 us -> 45.7 us  [local(): pl.pallas_call(wave_kernel, out_shape=(sds(pupils.shape, F32), sds((total...]
where the time goes in v1:
time: 73.6 us; the launch traced here: 73.3 us
  Pallas kernels  70.7 us (96%)
  local copies, waits for them, and re-layouts  1.34 us (2%)
    pallas_call x1, Pallas kernels, local(): pl.pallas_call(wave_kernel, out_shape=(sds(pupils.shape, F32), sds((total...  45.7 us
    pallas_call x1, Pallas kernels, local(): pl.pallas_call(finish_kernel, out_shape=(sds(spectrum.shape, BF16), sds(p...  18.9 us
    pallas_call x1, Pallas kernels, local(): pl.pallas_call(crop_kernel, out_shape=sds((total, 2, pw, pw), BF16), in_s...  6.12 us

profile of v1, /device:TPU:12, one launch (start us, length us, event | category | flops | bytes accessed | tf_op | source)
XLA Modules:
  0.0 73.3 jit_solution(11663179510141801894)
XLA Ops:
  0.6 0.6 add_convert_fusion.flag_ref
  1.2 0.8 %copy.9 = s32[1,2,4,2]{3,2,1,0:T(4,128)S(1)} copy(s32[1,2,4,2]{2,3,1,0:T(2,128)} %param.9) | data formatting | bytes 128 | tf_op args[3]
  2.0 0.6 reshape.10.start_ref
  2.6 6.1 %crops.1 = bf16[8,2,256,256]{3,2,1,0:T(8,128)(2,1)} custom-call(s32[16]{0:T(128)} %reshape.10.start_ref, s32[2]{0:T(128)} %bitcast.7, bf16[2,1152,2304]{2,1,0:T(8,128)(2,1)} %spec.5), custom_call_target="tpu_custom_call" | custom-call | tf_op jit(solution)/shard_map/crops/pallas_call | solution.py:577
  8.7 45.7 %waves.1 = (f32[2,256,512]{2,1,0:T(8,128)}, f32[8,2,256,256]{3,2,1,0:T(8,128)}, bf16[2,128,2304]{2,1,0:T(8,128)(2,1)}, bf16[2,128,2304]{2,1,0:T(8,128)(2,1)}, bf...) custom-call(s32[2]{0:T(128)} %bitcast.8, ...), custom_call_target="tpu_custom_call" | custom-call | tf_op jit(solution)/shard_map/waves/pallas_call | solution.py:593
  54.5 18.9 %finish.1 = (bf16[2,1152,2304]{2,1,0:T(8,128)(2,1)}, f32[2,256,512]{2,1,0:T(8,128)}) custom-call(s32[16]{0:T(128)} %reshape.10.start_ref, s32[2]{0:T(128)} %bitcast.9, f32[4]{0:T(128)} %add_convert_fusion.flag_ref, bf16[2,1152,2304]{2,1,0:T(8,128)(2,1)} %spec.5, f32[2,256,512]{2,1,0:T(8,128)} %get-tuple-element.16.pgrad_in, ...), custom_call_target="tpu_custom_call" | custom-call | tf_op jit(solution)/shard_map/finish/pallas_call | solution.py:615
